TPU v7x, 32 devices: a whole 2x2x4 slice. The times are simulated.
32 devices in a mesh: rows: 8 (over z, y), cols: 4 (over x, core).
Axes of the slice: x: 2, y: 2, z: 4, core: 2. Of those that a mesh axis runs over, the one named last changes fastest.
Arguments:
- slab: float32 [1536, 6144], P('rows', 'cols'), may hold values from -6 to 6
- factor: float32 [6144, 6144], P('cols', 'rows'), may hold values from -0.078125 to 0.078125
- block_inverse: float32 [6144, 1536], P('cols'), may hold values from -2 to 2, as said below
- pivot_order: int32 [6144], replicated, may hold values from 0 to 6143, as said below
- row_count: int32 [8], P('rows'), may hold values from 1 to 192, 1075 in all
Outputs:
- vectors: float32 [1536, 6144], P('rows', 'cols')
- mean_square: float32 [1536], P('rows')
Inputs may be any that keep to these rules, and one draw needn't show every extreme that they name: `pivot_order`: each of 0 to 6143 appears once. Of the 1536 pivots of one block, at most 768 have slab columns in any one block of 1536 slab columns, and exactly 768 in some. `row_count`: slots at or beyond the count hold entries that are ignored. `block_inverse`: each block of 1536 rows is lower triangular, with diagonal entries from 0.6 to 1.4.
All inputs are finite; a program needn't handle non-finite values. No bound on the sum of `row_count` on one device may be relied on, other than what follows from the above.
Results may differ from a plain program's by a relative error of at most 0.0001.
Values sent between devices are 32-bit elements; how exact they have to be, the bound alone decides.
A program may use at most 192 MiB of HBM per device.

v0:
```python
import functools
import jax
import jax.numpy as jnp
from jax import lax
from jax.experimental import pallas as pl
from jax.experimental.pallas import tpu as pltpu
from jax.sharding import PartitionSpec as P

MESH = pl.DeviceIdType.MESH


def times_transposed(left, right):
    return lax.dot_general(
        left,
        right,
        (((1,), (1,)), ((), ())),
        precision=lax.Precision.HIGH,
        preferred_element_type=jnp.float32,
    )


def gather_kernel(groups, side, chunks, part_ref, row_ref, mine, in_sem, keep_sem, right_sem, left_sem, hop_sem, side_sem, cross_sem):
    row, column = lax.axis_index("rows"), lax.axis_index("cols")
    a, b = row // side, row % side
    depth, width = part_ref.shape
    tall = depth // chunks

    def at(a_to, b_to):
        return (a_to * side + b_to, column)

    barrier = pltpu.get_barrier_semaphore()
    for step in (1, groups - 1):
        pl.semaphore_signal(barrier, inc=1, device_id=at((a + step) % groups, b), device_id_type=MESH)
    for step in range(1, side):
        pl.semaphore_signal(barrier, inc=1, device_id=at(a, (b + step) % side), device_id_type=MESH)
    pl.semaphore_wait(barrier, 2 + side - 1)

    def rows_of(i):
        return pl.ds(pl.multiple_of(i * tall, tall), tall)

    def place(k, b_of, i):
        return row_ref.at[k * side + b_of, rows_of(i), :]

    def right(k, i, source):
        return pltpu.make_async_remote_copy(source, place(k, b, i), right_sem.at[k, i], hop_sem.at[k, i], device_id=at(jnp.minimum(a + 1, groups - 1), b), device_id_type=MESH)

    def left(k, i, source):
        return pltpu.make_async_remote_copy(source, place(k, b, i), left_sem.at[k, i], hop_sem.at[k, i], device_id=at(jnp.maximum(a - 1, 0), b), device_id_type=MESH)

    def across(k, step, i, source):
        return pltpu.make_async_remote_copy(source, place(k, b, i), side_sem.at[step - 1, k, i], cross_sem.at[step - 1, k, i], device_id=at(a, (b + step) % side), device_id_type=MESH)

    def load(i):
        return pltpu.make_async_copy(part_ref.at[rows_of(i), :], mine.at[rows_of(i), :], in_sem.at[i])

    def keep(i):
        return pltpu.make_async_copy(mine.at[rows_of(i), :], place(a, b, i), keep_sem.at[i])

    @pl.when(a < column)
    def _():
        @pl.loop(0, chunks)
        def _(i):
            load(i).start()

        @pl.loop(0, chunks)
        def _(i):
            source = mine.at[rows_of(i), :]
            load(i).wait()

            @pl.when(a < groups - 1)
            def _():
                right(a, i, source).start()

            @pl.when(a > 0)
            def _():
                left(a, i, source).start()

            for step in range(1, side):
                across(a, step, i, source).start()
            keep(i).start()

    for hop in range(1, groups):
        @pl.loop(0, chunks)
        def _(i):
            k = a - hop

            @pl.when((k >= 0) & (k < column))
            def _():
                source = place(k, b, i)
                right(k, i, source).wait_recv()

                @pl.when(a < groups - 1)
                def _():
                    right(k, i, source).start()

                for step in range(1, side):
                    across(k, step, i, source).start()

            h = a + hop

            @pl.when((h <= groups - 1) & (h < column))
            def _():
                source = place(h, b, i)
                left(h, i, source).wait_recv()

                @pl.when(a > 0)
                def _():
                    left(h, i, source).start()

                for step in range(1, side):
                    across(h, step, i, source).start()

    for k in range(groups - 1):
        @pl.when(k < column)
        def _():
            @pl.loop(0, chunks)
            def _(i):
                source = place(k, b, i)
                for step in range(1, side):
                    came = place(k, (b + side - step) % side, i)
                    pltpu.make_async_remote_copy(came, came, side_sem.at[step - 1, k, i], cross_sem.at[step - 1, k, i], device_id=at(a, (b + step) % side), device_id_type=MESH).wait_recv()
                    across(k, step, i, source).wait_send()

                @pl.when((k <= a) & (a < groups - 1))
                def _():
                    right(k, i, source).wait_send()

                @pl.when((k >= a) & (a > 0))
                def _():
                    left(k, i, source).wait_send()

                @pl.when(k == a)
                def _():
                    keep(i).wait()


def gather_factor(factor, rows, groups):
    side = rows // groups
    depth, width = factor.shape
    chunks = max(1, depth // 256)
    sem = pltpu.SemaphoreType.DMA
    return pl.pallas_call(
        functools.partial(gather_kernel, groups, side, chunks),
        out_shape=jax.ShapeDtypeStruct(((groups - 1) * side, depth, width), jnp.float32),
        in_specs=[pl.BlockSpec(memory_space=pl.ANY)],
        out_specs=pl.BlockSpec(memory_space=pl.ANY),
        scratch_shapes=[
            pltpu.VMEM((depth, width), jnp.float32),
            sem((chunks,)),
            sem((chunks,)),
            sem((groups, chunks)),
            sem((groups, chunks)),
            sem((groups, chunks)),
            sem((side - 1, groups, chunks)),
            sem((side - 1, groups, chunks)),
        ],
        compiler_params=pltpu.CompilerParams(collective_id=0, has_side_effects=True, vmem_limit_bytes=58 * 1024 * 1024),
        cost_estimate=pl.CostEstimate(flops=0, bytes_accessed=600000000, transcendentals=0),
    )(factor)


def plain_device(slab, factor, block_inverse, pivot_order, row_count):
    rows_here, block_width = slab.shape
    row_devices = lax.axis_size("rows")
    column_count = lax.axis_size("cols")
    column = lax.axis_index("cols")
    total_width = block_width * column_count
    side = row_devices // column_count
    chosen = lax.dynamic_slice_in_dim(pivot_order, column * block_width, block_width)
    gathered = lax.all_gather(slab, "cols", axis=1, tiled=True)
    parts = gather_factor(factor, row_devices, column_count)
    gathered, parts = lax.optimization_barrier((gathered, parts))
    ordered = jnp.take(gathered, chosen, axis=1)
    live_rows = jnp.arange(rows_here, dtype=jnp.int32) < row_count[0]
    pending = jnp.where(live_rows[:, None], ordered, jnp.float32(0.0))

    def finish(values):
        return times_transposed(values, block_inverse)

    def nothing(values):
        return jnp.zeros_like(values)

    width = factor.shape[1]
    vectors = jnp.zeros_like(pending)
    for k in range(column_count):
        finished = lax.cond(column == k, finish, nothing, pending)
        vectors = vectors + finished
        if k + 1 < column_count:
            arrived = moving = finished
            for to in range(k + 1, column_count):
                moving = lax.ppermute(moving, "cols", [(to - 1, to)])
                arrived = jnp.where(column == to, moving, arrived)
            update = jnp.zeros_like(pending)
            for b in range(side):
                update += times_transposed(arrived[:, b * width : (b + 1) * width], parts[k * side + b])
            pending = pending - jnp.where(k < column, update, jnp.float32(0.0))
    row_sums = lax.psum(jnp.sum(vectors * vectors, axis=1), "cols")
    return (vectors, row_sums / total_width)


TALL = 128
WIDE = 256
ROUND = 64
LAG = 2


def target_of(j, k):
    if k == j - 1:
        return j if j % 2 else j - 2
    return j - 1 if j % 2 and k == 0 else None


def halves(values):
    high = values.astype(jnp.bfloat16)
    return high, (values - high.astype(jnp.float32)).astype(jnp.bfloat16)


def nt(left, right):
    return lax.dot_general(left, right, (((1,), (1,)), ((), ())), preferred_element_type=jnp.float32)


def nt3(stacked, right):
    rows = stacked.shape[0] // 2
    high, low = halves(right)
    both = nt(stacked, high)
    return both[:rows] + (both[rows:] + nt(stacked[:rows], low))


def chain_kernel(
    groups,
    side,
    slab_ref,
    factor_ref,
    inverse_ref,
    order_ref,
    live_ref,
    out_ref,
    mean_ref,
    buf,
    inverse,
    slabs,
    rest,
    vec,
    stack,
    vec_in,
    part_in,
    part_out,
    sums,
    ones,
    stay,
    guest,
    guest_stack,
    guest_part,
    load_sem,
    recv_sem,
    up_sem,
    down_sem,
    side_sem,
    entry_sem,
    inverse_sem,
    own_sem,
    slab_send,
    slab_recv,
    pass_send,
    vec_send,
    vec_recv,
    part_send,
    part_recv,
    sum_send,
    sum_recv,
    out_sem,
    stay_load,
    stay_send,
    stay_recv,
    guest_send,
    guest_recv,
    back_send,
    back_recv,
):
    columns = groups
    row, column = lax.axis_index("rows"), lax.axis_index("cols")
    a, b = row // side, row % side
    height, width = rest.shape
    depth, part = factor_ref.shape
    chunks = depth // TALL
    pieces = width // WIDE
    rounds = height // ROUND
    chips = columns // 2
    chip, core = column // 2, column % 2
    all_blocks = [(j, k) for j in range(1, columns) for k in range(j)]
    moving = [jk for jk in all_blocks if target_of(*jk) is not None]
    staying = [jk for jk in all_blocks if target_of(*jk) is None]
    blocks = [[jk for jk in moving if target_of(*jk) == c] for c in range(columns)]
    before = [[jk for jk in blocks[c] if jk[1] < c] for c in range(columns)]
    after = [[jk for jk in blocks[c] if jk[1] > c] for c in range(columns)]
    vec_from = [sorted({k for _, k in blocks[c] if k != c}) for c in range(columns)]
    vec_to = [[u for u in range(columns) if c in vec_from[u]] for c in range(columns)]
    part_from = [[k for k in range(c) if target_of(c, k) != c] for c in range(columns)]
    part_made = [[jk for jk in blocks[c] if jk[0] != c] for c in range(columns)]

    def there(c):
        return (row, c)

    def level(z, c):
        return (z * side + b, c)

    def beside(step):
        return (a * side + (b + step) % side, column)

    def remote(source, target, send, recv, device):
        return pltpu.make_async_remote_copy(source, target, send, recv, device_id=device, device_id_type=MESH)

    def landed(here, recv):
        remote(here, here, out_sem, recv, there(column)).wait_recv()

    def tall(i):
        return pl.ds(pl.multiple_of(i * TALL, TALL), TALL)

    def wide(q):
        return pl.ds(pl.multiple_of(q * WIDE, WIDE), WIDE)

    def few(r):
        return pl.ds(pl.multiple_of(r * ROUND, ROUND), ROUND)

    def on(c, work):
        pl.when(column == c)(work)

    barrier = pltpu.get_barrier_semaphore()
    for step in range(1, side):
        pl.semaphore_signal(barrier, inc=1, device_id=beside(step), device_id_type=MESH)
    for up_by in range(groups):
        for right_by in range(columns):
            if up_by or right_by:
                pl.semaphore_signal(barrier, inc=1, device_id=level((a + up_by) % groups, (column + right_by) % columns), device_id_type=MESH)
    pl.semaphore_wait(barrier, side - 1 + groups * columns - 1)

    def source_of(d, f):
        return (chip + d) % chips * 2 + (core + f) % 2

    partner = source_of(0, 1)
    own_load = pltpu.make_async_copy(slab_ref, slabs.at[column], own_sem)
    own_load.start()
    inverse_load = pltpu.make_async_copy(inverse_ref, inverse, inverse_sem)

    def slab_out(d):
        to = source_of(d, 0) if d else partner
        return remote(slab_ref, slabs.at[column], slab_send.at[d], slab_recv.at[column], there(to))

    def slab_pass(d):
        place = slabs.at[source_of(d, 0)]
        return remote(place, place, pass_send.at[d - 1], slab_recv.at[source_of(d, 0)], there(partner))

    for d in list(range(1, chips)) + [0]:
        slab_out(d).start()

    def place(slot, half, i):
        return buf.at[slot, half, tall(i), :]

    def load(slot, i):
        return pltpu.make_async_copy(factor_ref.at[tall(i), :], place(slot, b, i), load_sem.at[i])

    def entry(slot, i, to):
        return remote(factor_ref.at[tall(i), :], place(slot, b, i), entry_sem.at[i], recv_sem.at[slot, b, i], there(to))

    def up(slot, i):
        return remote(place(slot, b, i), place(slot, b, i), up_sem.at[slot, i], recv_sem.at[slot, b, i], level(jnp.minimum(a + 1, groups - 1), column))

    def down(slot, half, i):
        return remote(place(slot, half, i), place(slot, half, i), down_sem.at[slot, half, i], recv_sem.at[slot, half, i], level(jnp.maximum(a - 1, 0), column))

    def across(slot, step, i):
        return remote(place(slot, b, i), place(slot, b, i), side_sem.at[step - 1, slot, i], recv_sem.at[slot, b, i], beside(step))

    def arrived(slot, half, i):
        landed(place(slot, half, i), recv_sem.at[slot, half, i])

    def both_down(block):
        return block[1] >= 2

    def flows(slot, block, i, act):
        k = block[1]

        @pl.when((a >= k) & (a < groups - 1))
        def _():
            act(up(slot, i))

        @pl.when((a <= k) & (a > 0))
        def _():
            act(down(slot, b, i))

        if both_down(block):

            @pl.when(a >= k)
            def _():
                for step in range(1, side):
                    act(across(slot, step, i))
        else:
            for step in range(1, side):
                act(across(slot, step, i))

    def other_flows(slot, block, i, act):
        @pl.when((a <= block[1]) & (a > 0))
        def _():
            for step in range(1, side):
                act(down(slot, (b + step) % side, i))

    def serve(slot, block, i):
        j, k = block
        if target_of(j, k) == j:

            @pl.when(a == k)
            def _():
                load(slot, i).wait()

            @pl.when(a != k)
            def _():
                arrived(slot, b, i)
        else:
            arrived(slot, b, i)
        flows(slot, block, i, lambda copy: copy.start())
        if both_down(block):

            @pl.when(i >= LAG)
            def _():
                serve_others(slot, block, i - LAG)

    def serve_others(slot, block, i):
        for step in range(1, side):
            arrived(slot, (b + step) % side, i)
        other_flows(slot, block, i, lambda copy: copy.start())

    def others(slot, block, i):
        if not both_down(block):
            for step in range(1, side):
                arrived(slot, (b + step) % side, i)

    def stay_out(step, q):
        return remote(factor_ref.at[wide(q), :], stay.at[b, wide(q), :], stay_send.at[step - 1, q], stay_recv.at[b, q], beside(step))

    def stay_in():
        return pltpu.make_async_copy(factor_ref, stay.at[b], stay_load)

    for j, k in all_blocks:
        t = target_of(j, k)

        @pl.when((column == j) & (a == k))
        def _():
            if t is None:
                for q in range(pieces):
                    for step in range(1, side):
                        stay_out(step, q).start()
                stay_in().start()
            else:
                slot = blocks[t].index((j, k))

                @pl.loop(0, chunks)
                def _(i):
                    if t == j:
                        load(slot, i).start()
                    else:
                        entry(slot, i, t).start()

    inverse_load.start()

    rest[...] = jnp.zeros_like(rest)
    ones[...] = jnp.ones_like(ones)
    for turn in range(columns):
        d, f = turn // 2, turn % 2
        s = source_of(d, f)
        for c in range(columns):
            low, high = turn * chunks // columns, (turn + 1) * chunks // columns
            if before[c] and high > low:

                def work(c=c, low=low, high=high):
                    @pl.loop(low, high)
                    def _(i):
                        for block in before[c]:
                            serve(blocks[c].index(block), block, i)

                on(c, work)
        if turn == 0:
            own_load.wait()
        else:
            landed(slabs.at[s], slab_recv.at[s])
            if f == 0:
                slab_pass(d).start()
        high, low = halves(slabs[s] * live_ref[...])
        stack[:height] = high
        stack[height:] = low

        @pl.loop(0, pieces)
        def _(q):
            index = lax.broadcasted_iota(jnp.int32, (width, WIDE), 0) + s * width
            chosen = jnp.where(index == order_ref[:, wide(q)], 1.0, 0.0).astype(jnp.bfloat16)
            both = jnp.dot(stack[...], chosen, preferred_element_type=jnp.float32)
            rest[:, wide(q)] += both[:height] + both[height:]

    def finish_serving(c):
        for block in before[c]:
            if both_down(block):

                @pl.loop(chunks - LAG, chunks)
                def _(i):
                    serve_others(blocks[c].index(block), block, i)

    def vec_wait(slot, q):
        landed(vec_in.at[slot, :, wide(q)], vec_recv.at[slot, q])

    def part_wait(slot, q):
        landed(part_in.at[slot, :, wide(q)], part_recv.at[slot, q])

    def vec_out(c, n, q):
        u = vec_to[c][n]
        slot = vec_from[u].index(c)
        return remote(vec.at[:, wide(q)], vec_in.at[slot, :, wide(q)], vec_send.at[n, q], vec_recv.at[slot, q], there(u))

    def part_to(block, made, q):
        j, k = block
        slot = part_from[j].index(k)
        return remote(part_out.at[made, :, wide(q)], part_in.at[slot, :, wide(q)], part_send.at[made, q], part_recv.at[slot, q], there(j))

    def put(values):
        high, low = halves(values)
        stack[:height] = high
        stack[height:] = low

    def known(j, k):
        return k in vec_from[j]

    def guest_out(n, j, k, r):
        return remote(vec.at[few(r), :], guest.at[a, few(r), :], guest_send.at[n, r], guest_recv.at[a, r], level(k, j))

    def back(j, k, z, r):
        slot = part_from[j].index(k)
        source = guest_part.at[r, z * ROUND : (z + 1) * ROUND, :]
        return remote(source, part_in.at[slot, few(r), :], back_send.at[z, r], back_recv.at[slot, r], level(z, j))

    def host(j, k):
        slot = part_from[j].index(k)
        if known(j, k):
            for q in range(pieces):
                vec_wait(vec_from[j].index(k), q)
        stay_in().wait()
        for step in range(1, side):
            half = (b + step) % side
            for q in range(pieces):
                landed(stay.at[half, wide(q), :], stay_recv.at[half, q])

        @pl.loop(0, rounds)
        def _(r):
            for z in range(groups):
                if z == k and known(j, k):
                    high, low = halves(vec_in[vec_from[j].index(k), few(r), :])
                else:
                    landed(guest.at[z, few(r), :], guest_recv.at[z, r])
                    high, low = halves(guest[z, few(r), :])
                guest_stack[z * ROUND : (z + 1) * ROUND] = high
                guest_stack[(groups + z) * ROUND : (groups + z + 1) * ROUND] = low

            @pl.loop(0, pieces)
            def _(q):
                total = jnp.zeros((groups * ROUND, WIDE), jnp.float32)
                for half in range(side):
                    total += nt3(guest_stack[:, half * part : (half + 1) * part], stay[half, wide(q), :])
                guest_part[r, :, wide(q)] = total
                part_in[slot, few(r), wide(q)] = total[k * ROUND : (k + 1) * ROUND]

            for z in range(groups):
                if z != k:
                    back(j, k, z, r).start()

    def make_part(c, block, q):
        slot, made = blocks[c].index(block), part_made[c].index(block)
        for n in range(WIDE // TALL):
            others(slot, block, q * (WIDE // TALL) + n)
        total = jnp.zeros((height, WIDE), jnp.float32)
        for half in range(side):
            total += nt3(stack[:, half * part : (half + 1) * part], buf[slot, half, wide(q), :])
        part_out[made, :, wide(q)] = total
        part_to(block, made, q).start()

    def take_before(c):
        finish_serving(c)
        for j, k in staying:
            if j == c:
                pl.when(a == k)(functools.partial(host, j, k))
        for block in before[c]:
            j, k = block
            slot, coming = blocks[c].index(block), vec_from[c].index(k)
            if j != c:

                def work(k=k):
                    for q in range(pieces):
                        vec_wait(coming, q)

                if known(c, k) and (c, k) in staying:
                    pl.when(a != k)(work)
                else:
                    work()
                put(vec_in[coming])

                @pl.loop(0, pieces)
                def _(q):
                    make_part(c, block, q)
            else:

                @pl.loop(0, chunks)
                def _(i):
                    others(slot, block, i)

                for q in range(pieces):
                    vec_wait(coming, q)
                    high, low = halves(vec_in[coming, :, q * WIDE : (q + 1) * WIDE])
                    stack[:height, :WIDE] = high
                    stack[height:, :WIDE] = low
                    half, at = q * WIDE // part, q * WIDE % part

                    @pl.loop(0, pieces)
                    def _(n):
                        rest[:, wide(n)] -= nt3(stack[:, :WIDE], buf[slot, half, wide(n), at : at + WIDE])

    for c in range(columns):
        if before[c]:
            on(c, functools.partial(take_before, c))

    inverse_load.wait()
    squares = jnp.zeros((8, height), jnp.float32)
    for q in range(pieces):
        here = slice(q * WIDE, (q + 1) * WIDE)
        for c in range(columns):
            if part_from[c]:

                def work(c=c):
                    for slot, k in enumerate(part_from[c]):
                        if (c, k) not in staying:
                            part_wait(slot, q)
                        elif q == 0:

                            @pl.when(a != k)
                            def _():
                                for r in range(rounds):
                                    landed(part_in.at[slot, few(r), :], back_recv.at[slot, r])

                        rest[:, here] -= part_in[slot, :, here]

                on(c, work)
        high, low = halves(rest[:, here])
        stack[:height, here] = high
        stack[height:, here] = low
        done = nt3(stack[:, : (q + 1) * WIDE], inverse[here, : (q + 1) * WIDE])
        vec[:, here] = done
        high, low = halves(done * done)
        squares += nt(ones[...], high) + nt(ones[...], low)
        for c in range(columns):
            if vec_to[c]:

                def work(c=c):
                    for n in range(len(vec_to[c])):
                        vec_out(c, n, q).start()

                on(c, work)

    def guests(c, act):
        for n, (j, k) in enumerate([jk for jk in staying if jk[1] == c]):

            def work():
                for r in range(rounds):
                    act(guest_out(n, j, k, r))

            if known(j, k):
                pl.when(a != k)(work)
            else:
                work()

    for c in range(columns):
        on(c, functools.partial(guests, c, lambda copy: copy.start()))
    store = pltpu.make_async_copy(vec, out_ref, out_sem)
    store.start()
    sums[column] = squares

    def sum_out(step):
        to = (column + step) % columns
        return remote(sums.at[column], sums.at[column], sum_send.at[step - 1], sum_recv.at[column], there(to))

    for step in range(1, columns):
        sum_out(step).start()

    def give_after(c):
        for block in after[c]:
            slot, coming = blocks[c].index(block), vec_from[c].index(block[1])

            @pl.loop(0, chunks - pieces)
            def _(i):
                serve(slot, block, i)

            for q in range(pieces):
                vec_wait(coming, q)
            put(vec_in[coming])

            @pl.loop(0, pieces)
            def _(q):
                serve(slot, block, chunks - pieces + q)
                make_part(c, block, q)

    for c in range(columns):
        if after[c]:
            on(c, functools.partial(give_after, c))

    for d in range(chips):
        slab_out(d).wait_send()
    for d in range(1, chips):
        slab_pass(d).wait_send()
    for j, k in all_blocks:
        t = target_of(j, k)

        @pl.when((column == j) & (a == k))
        def _():
            if t is None:
                for q in range(pieces):
                    for step in range(1, side):
                        stay_out(step, q).wait_send()
                for r in range(rounds):
                    for z in range(groups):
                        if z != k:
                            back(j, k, z, r).wait_send()
            elif t != j:

                @pl.loop(0, chunks)
                def _(i):
                    entry(blocks[t].index((j, k)), i, t).wait_send()

    for c in range(columns):

        def work(c=c):
            for slot, block in enumerate(blocks[c]):

                @pl.loop(0, chunks)
                def _(i):
                    flows(slot, block, i, lambda copy: copy.wait_send())
                    if both_down(block):
                        other_flows(slot, block, i, lambda copy: copy.wait_send())

            for q in range(pieces):
                for n in range(len(vec_to[c])):
                    vec_out(c, n, q).wait_send()
                for made, block in enumerate(part_made[c]):
                    part_to(block, made, q).wait_send()
            guests(c, lambda copy: copy.wait_send())

        on(c, work)
    for step in range(1, columns):
        came = (column + step) % columns
        landed(sums.at[came], sum_recv.at[came])
    total = sums[0]
    for c in range(1, columns):
        total += sums[c]
    mean_ref[...] = total[:1] / (width * columns)
    for step in range(1, columns):
        sum_out(step).wait_send()
    store.wait()


def chain_device(slab, factor, block_inverse, pivot_order, row_count):
    height, width = slab.shape
    depth, part = factor.shape
    groups = lax.axis_size("cols")
    side = lax.axis_size("rows") // groups
    column = lax.axis_index("cols")
    order = lax.dynamic_slice_in_dim(pivot_order, column * width, width)[None, :]
    live = (jnp.arange(height, dtype=jnp.int32) < row_count[0]).astype(jnp.float32)[:, None]
    slots = max([sum(target_of(j, k) == c for j in range(groups) for k in range(j)) for c in range(groups)])
    chunks, pieces, rounds, chips = depth // TALL, width // WIDE, height // ROUND, groups // 2
    sem, space = pltpu.SemaphoreType.DMA, pltpu.VMEM
    f32, bf16 = jnp.float32, jnp.bfloat16
    held = pl.BlockSpec(memory_space=pltpu.VMEM)
    away = pl.BlockSpec(memory_space=pl.ANY)
    vectors, mean = pl.pallas_call(
        functools.partial(chain_kernel, groups, side),
        out_shape=(jax.ShapeDtypeStruct((height, width), f32), jax.ShapeDtypeStruct((1, height), f32)),
        in_specs=[away, away, away, held, held],
        out_specs=(away, held),
        scratch_shapes=[
            space((slots, side, depth, part), f32),
            space((width, width), f32),
            space((groups, height, width), f32),
            space((height, width), f32),
            space((height, width), f32),
            space((2 * height, width), bf16),
            space((1, height, width), f32),
            space((groups - 2, height, width), f32),
            space((1, height, width), f32),
            space((groups, 8, height), f32),
            space((8, WIDE), bf16),
            space((side, depth, part), f32),
            space((groups, height, width), f32),
            space((2 * groups * ROUND, width), bf16),
            space((rounds, groups * ROUND, width), f32),
            sem((chunks,)),
            sem((slots, side, chunks)),
            sem((slots, chunks)),
            sem((slots, side, chunks)),
            sem((side - 1, slots, chunks)),
            sem((chunks,)),
            sem(()),
            sem(()),
            sem((chips,)),
            sem((groups,)),
            sem((chips - 1,)),
            sem((groups, pieces)),
            sem((groups, pieces)),
            sem((groups, pieces)),
            sem((groups, pieces)),
            sem((groups,)),
            sem((groups,)),
            sem(()),
            sem(()),
            sem((side - 1, pieces)),
            sem((side, pieces)),
            sem((groups, rounds)),
            sem((groups, rounds)),
            sem((groups, rounds)),
            sem((groups, rounds)),
        ],
        compiler_params=pltpu.CompilerParams(collective_id=0, has_side_effects=True, vmem_limit_bytes=60 * 1024 * 1024),
    )(slab, factor, block_inverse, order, live)
    return vectors, mean[0]


def per_device(slab, factor, block_inverse, pivot_order, row_count):
    groups, rows = lax.axis_size("cols"), lax.axis_size("rows")
    depth, part = factor.shape
    fits = groups // 2 == 2 and rows % groups == 0 and rows > groups and part % WIDE == 0 and depth % WIDE == 0 and slab.shape[0] % ROUND == 0
    one = chain_device if fits else plain_device
    return one(slab, factor, block_inverse, pivot_order, row_count)


def solution(mesh):
    placed = (P("rows", "cols"), P("cols", "rows"), P("cols", None), P(), P("rows"))
    return jax.shard_map(
        per_device,
        mesh=mesh,
        in_specs=placed,
        out_specs=(P("rows", "cols"), P("rows")),
        check_vma=False,
    )
```

profile of v0, /device:TPU:0, one launch (start us, length us, event | category | flops | bytes accessed | tf_op | source)
XLA Modules:
  0.0 183.5 jit_solution(12290579250562054898)
XLA Ops:
  1.3 0.8 dynamic_slice.3
  2.1 0.6 broadcast_in_dim.4.order_ref
  2.7 0.7 fusion.live_ref
  3.3 177.2 %shard_map.68 = (f32[192,1536]{1,0:T(8,128)}, f32[1,192]{1,0:T(1,128)}) custom-call(f32[192,1536]{1,0:T(8,128)} %slab_ref.1, f32[1536,768]{1,0:T(8,128)} %factor_ref.1, f32[1536,1536]{1,0:T(8,128)} %inverse_ref.1, s32[1,1536]{1,0:T(1,128)} %broadcast_in_dim.4.order_ref, f32[192,1]{1,0:T(8,128)} %fusion.live_ref), custom_call_target="tpu_custom_call" | custom-call | tf_op jit(solution)/shard_map/pallas_call | solution.py:777
  180.6 0.0 copy-start
  180.6 2.4 %copy.10 = f32[192,1536]{1,0:T(8,128)} copy(f32[192,1536]{1,0:T(8,128)} %get-tuple-element.8) | data formatting | bytes 2359296
  182.9 0.0 copy-done
  182.9 0.6 copy.11
Async XLA Ops:
  180.6 2.4 %copy-start = (f32[1,192]{1,0:T(1,128)S(1)}, f32[1,192]{1,0:T(1,128)}, u32[]{:S(2)}) copy-start(f32[1,192]{1,0:T(1,128)} %get-tuple-element.5) | copy-start | bytes 2308
where the time goes:
time: 184 us
  Pallas kernels  177 us (96%)
  local copies, waits for them, and re-layouts  4.31 us (2%)
    pallas_call x1, Pallas kernels, chain_device(): pl.pallas_call(functools.partial(chain_kernel, groups, side), out_shape=(...  177 us

commit v1 on v0

--- a/solution.py
+++ b/solution.py
@@ -200,14 +200,18 @@
 
 TALL = 128
 WIDE = 256
-ROUND = 64
-LAG = 2
+EARLY = (5, 7, 9)
+LATER = 4
 
 
 def target_of(j, k):
     if k == j - 1:
         return j if j % 2 else j - 2
     return j - 1 if j % 2 and k == 0 else None
+
+
+def host_of(j, k):
+    return j - 1 if j % 2 else j
 
 
 def halves(values):
@@ -276,6 +280,9 @@
     guest_recv,
     back_send,
     back_recv,
+    lift_send,
+    lift_back_send,
+    gate,
 ):
     columns = groups
     row, column = lax.axis_index("rows"), lax.axis_index("cols")
@@ -284,7 +291,8 @@
     depth, part = factor_ref.shape
     chunks = depth // TALL
     pieces = width // WIDE
-    rounds = height // ROUND
+    rounds = groups - 1
+    share = height // rounds
     chips = columns // 2
     chip, core = column // 2, column % 2
     all_blocks = [(j, k) for j in range(1, columns) for k in range(j)]
@@ -293,6 +301,8 @@
     blocks = [[jk for jk in moving if target_of(*jk) == c] for c in range(columns)]
     before = [[jk for jk in blocks[c] if jk[1] < c] for c in range(columns)]
     after = [[jk for jk in blocks[c] if jk[1] > c] for c in range(columns)]
+    heir = [host_of(*[jk for jk in staying if jk[1] == k][0]) if [jk for jk in staying if jk[1] == k] else None for k in range(columns)]
+    hosted = [[k for j, k in staying if host_of(j, k) == c] for c in range(columns)]
     vec_from = [sorted({k for _, k in blocks[c] if k != c}) for c in range(columns)]
     vec_to = [[u for u in range(columns) if c in vec_from[u]] for c in range(columns)]
     part_from = [[k for k in range(c) if target_of(c, k) != c] for c in range(columns)]
@@ -320,7 +330,7 @@
         return pl.ds(pl.multiple_of(q * WIDE, WIDE), WIDE)
 
     def few(r):
-        return pl.ds(pl.multiple_of(r * ROUND, ROUND), ROUND)
+        return pl.ds(pl.multiple_of(r * share, share), share)
 
     def on(c, work):
         pl.when(column == c)(work)
@@ -328,11 +338,13 @@
     barrier = pltpu.get_barrier_semaphore()
     for step in range(1, side):
         pl.semaphore_signal(barrier, inc=1, device_id=beside(step), device_id_type=MESH)
+        for right_by in range(1, columns):
+            pl.semaphore_signal(barrier, inc=1, device_id=(a * side + (b + step) % side, (column + right_by) % columns), device_id_type=MESH)
     for up_by in range(groups):
         for right_by in range(columns):
             if up_by or right_by:
                 pl.semaphore_signal(barrier, inc=1, device_id=level((a + up_by) % groups, (column + right_by) % columns), device_id_type=MESH)
-    pl.semaphore_wait(barrier, side - 1 + groups * columns - 1)
+    pl.semaphore_wait(barrier, (side - 1) * columns + groups * columns - 1)
 
     def source_of(d, f):
         return (chip + d) % chips * 2 + (core + f) % 2
@@ -377,20 +389,29 @@
     def both_down(block):
         return block[1] >= 2
 
-    def flows(slot, block, i, act):
+    def lifted(block):
+        return block[0] % 2 == 0
+
+    def free_level(block):
+        return functools.reduce(jnp.logical_and, [a != k for k in hosted[target_of(*block)]], a >= 0)
+
+    def line_flows(slot, block, i, act):
         k = block[1]
 
         @pl.when((a >= k) & (a < groups - 1))
         def _():
             act(up(slot, i))
 
-        @pl.when((a <= k) & (a > 0))
-        def _():
-            act(down(slot, b, i))
-
-        if both_down(block):
-
-            @pl.when(a >= k)
+        if not lifted(block):
+
+            @pl.when((a <= k) & (a > 0))
+            def _():
+                act(down(slot, b, i))
+
+    def side_flows(slot, block, i, act):
+        if both_down(block) or lifted(block):
+
+            @pl.when(a >= block[1])
             def _():
                 for step in range(1, side):
                     act(across(slot, step, i))
@@ -417,12 +438,20 @@
                 arrived(slot, b, i)
         else:
             arrived(slot, b, i)
-        flows(slot, block, i, lambda copy: copy.start())
-        if both_down(block):
-
-            @pl.when(i >= LAG)
-            def _():
-                serve_others(slot, block, i - LAG)
+        line_flows(slot, block, i, lambda copy: copy.start())
+
+        @pl.when(free_level(block))
+        def _():
+            side_flows(slot, block, i, lambda copy: copy.start())
+
+
+    def serve_ahead(slot, block, q, ahead):
+        for n in range(WIDE // TALL):
+            i = ahead + q * (WIDE // TALL) + n
+
+            @pl.when(i < chunks)
+            def _():
+                serve(slot, block, i)
 
     def serve_others(slot, block, i):
         for step in range(1, side):
@@ -430,12 +459,17 @@
         other_flows(slot, block, i, lambda copy: copy.start())
 
     def others(slot, block, i):
-        if not both_down(block):
+        def work():
             for step in range(1, side):
                 arrived(slot, (b + step) % side, i)
 
-    def stay_out(step, q):
-        return remote(factor_ref.at[wide(q), :], stay.at[b, wide(q), :], stay_send.at[step - 1, q], stay_recv.at[b, q], beside(step))
+        if both_down(block):
+            pl.when((a > block[1]) | (a == 0))(work)
+        else:
+            work()
+
+    def stay_out(step, q, to):
+        return remote(factor_ref.at[wide(q), :], stay.at[b, wide(q), :], stay_send.at[step, q], stay_recv.at[b, q], (a * side + (b + step) % side, to))
 
     def stay_in():
         return pltpu.make_async_copy(factor_ref, stay.at[b], stay_load)
@@ -446,10 +480,11 @@
         @pl.when((column == j) & (a == k))
         def _():
             if t is None:
-                for q in range(pieces):
-                    for step in range(1, side):
-                        stay_out(step, q).start()
-                stay_in().start()
+                for step in range(0 if host_of(j, k) != j else 1, side):
+                    for q in range(pieces):
+                        stay_out(step, q, host_of(j, k)).start()
+                if host_of(j, k) == j:
+                    stay_in().start()
             else:
                 slot = blocks[t].index((j, k))
 
@@ -464,20 +499,40 @@
 
     rest[...] = jnp.zeros_like(rest)
     ones[...] = jnp.ones_like(ones)
+
+    def serving(c, low, high):
+        for block in before[c]:
+
+            def work(block=block):
+                @pl.loop(low(block), high(block))
+                def _(i):
+                    serve(blocks[c].index(block), block, i)
+
+            pl.when(a != block[1])(work)
+
+    def early(n):
+        return lambda block: jnp.maximum(EARLY[n] - jnp.abs(a - block[1]), 0)
+
+    def serve_source(c):
+        for block in before[c]:
+
+            def work(block=block):
+                @pl.loop(0, chunks)
+                def _(i):
+                    serve(blocks[c].index(block), block, i)
+
+            pl.when(a == block[1])(work)
+
+    for c in range(columns):
+        if before[c]:
+            on(c, functools.partial(serve_source, c))
     for turn in range(columns):
         d, f = turn // 2, turn % 2
         s = source_of(d, f)
-        for c in range(columns):
-            low, high = turn * chunks // columns, (turn + 1) * chunks // columns
-            if before[c] and high > low:
-
-                def work(c=c, low=low, high=high):
-                    @pl.loop(low, high)
-                    def _(i):
-                        for block in before[c]:
-                            serve(blocks[c].index(block), block, i)
-
-                on(c, work)
+        if turn >= 2:
+            for c in range(columns):
+                if before[c]:
+                    on(c, functools.partial(serving, c, early(turn - 3) if turn > 2 else lambda block: 0, early(turn - 2)))
         if turn == 0:
             own_load.wait()
         else:
@@ -495,14 +550,6 @@
             both = jnp.dot(stack[...], chosen, preferred_element_type=jnp.float32)
             rest[:, wide(q)] += both[:height] + both[height:]
 
-    def finish_serving(c):
-        for block in before[c]:
-            if both_down(block):
-
-                @pl.loop(chunks - LAG, chunks)
-                def _(i):
-                    serve_others(blocks[c].index(block), block, i)
-
     def vec_wait(slot, q):
         landed(vec_in.at[slot, :, wide(q)], vec_recv.at[slot, q])
 
@@ -514,6 +561,30 @@
         slot = vec_from[u].index(c)
         return remote(vec.at[:, wide(q)], vec_in.at[slot, :, wide(q)], vec_send.at[n, q], vec_recv.at[slot, q], there(u))
 
+    def vec_outs(c, q, act):
+        for n, u in enumerate(vec_to[c]):
+            lifting = [jk for jk in after[u] if jk[1] == c]
+
+            def work():
+                act(vec_out(c, n, q))
+
+            if lifting:
+                pl.when(a >= c)(work)
+            else:
+                work()
+
+    def lift_to(c):
+        return [jk for u in range(columns) for jk in after[u] if jk[1] == c]
+
+    def lift_out(block, r):
+        j, k = block
+        return remote(vec.at[few(r), :], guest.at[a, few(r), :], lift_send.at[r], guest_recv.at[a, r], level(k, target_of(j, k)))
+
+    def lift_back(block, z, q):
+        j, k = block
+        slot = part_from[j].index(k)
+        return remote(guest.at[groups - 1 - z, :, wide(q)], part_in.at[slot, :, wide(q)], lift_back_send.at[z, q], part_recv.at[slot, q], level(z, j))
+
     def part_to(block, made, q):
         j, k = block
         slot = part_from[j].index(k)
@@ -524,50 +595,83 @@
         stack[:height] = high
         stack[height:] = low
 
-    def known(j, k):
-        return k in vec_from[j]
-
-    def guest_out(n, j, k, r):
-        return remote(vec.at[few(r), :], guest.at[a, few(r), :], guest_send.at[n, r], guest_recv.at[a, r], level(k, j))
+    def known(k):
+        return k in vec_from[heir[k]]
+
+    def guest_out(k, r):
+        return remote(vec.at[few(r), :], guest.at[a, few(r), :], guest_send.at[r], guest_recv.at[a, r], level(k, heir[k]))
 
     def back(j, k, z, r):
         slot = part_from[j].index(k)
-        source = guest_part.at[r, z * ROUND : (z + 1) * ROUND, :]
+        n = z - (z > k)
+        source = guest_part.at[r, n * share : (n + 1) * share, :] if z != k else guest_part.at[rounds, few(r), :]
         return remote(source, part_in.at[slot, few(r), :], back_send.at[z, r], back_recv.at[slot, r], level(z, j))
 
+    def products(rows, q):
+        total = jnp.zeros((rows, WIDE), jnp.float32)
+        for half in range(side):
+            total += nt3(guest_stack[:, half * part : (half + 1) * part], stay[half, wide(q), :])
+        return total
+
     def host(j, k):
-        slot = part_from[j].index(k)
-        if known(j, k):
-            for q in range(pieces):
-                vec_wait(vec_from[j].index(k), q)
-        stay_in().wait()
-        for step in range(1, side):
+        c = host_of(j, k)
+        if c == j:
+            stay_in().wait()
+        for step in range(1 if c == j else 0, side):
             half = (b + step) % side
             for q in range(pieces):
                 landed(stay.at[half, wide(q), :], stay_recv.at[half, q])
+        for block in blocks[c]:
+
+            @pl.loop(0, chunks)
+            def _(i):
+                side_flows(blocks[c].index(block), block, i, lambda copy: copy.start())
+
+        away = [z for z in range(groups) if z != k]
+        tall_of = len(away) * share
 
         @pl.loop(0, rounds)
         def _(r):
-            for z in range(groups):
-                if z == k and known(j, k):
-                    high, low = halves(vec_in[vec_from[j].index(k), few(r), :])
-                else:
-                    landed(guest.at[z, few(r), :], guest_recv.at[z, r])
-                    high, low = halves(guest[z, few(r), :])
-                guest_stack[z * ROUND : (z + 1) * ROUND] = high
-                guest_stack[(groups + z) * ROUND : (groups + z + 1) * ROUND] = low
+            for n, z in enumerate(away):
+                landed(guest.at[z, few(r), :], guest_recv.at[z, r])
+                high, low = halves(guest[z, few(r), :])
+                guest_stack[n * share : (n + 1) * share] = high
+                guest_stack[tall_of + n * share : tall_of + (n + 1) * share] = low
 
             @pl.loop(0, pieces)
             def _(q):
-                total = jnp.zeros((groups * ROUND, WIDE), jnp.float32)
-                for half in range(side):
-                    total += nt3(guest_stack[:, half * part : (half + 1) * part], stay[half, wide(q), :])
-                guest_part[r, :, wide(q)] = total
-                part_in[slot, few(r), wide(q)] = total[k * ROUND : (k + 1) * ROUND]
-
-            for z in range(groups):
-                if z != k:
-                    back(j, k, z, r).start()
+                guest_part[r, :, wide(q)] = products(tall_of, q)
+
+            for n, z in enumerate(away):
+                back(j, k, z, r).start()
+
+        if c == j:
+            host_own(j, k)
+
+    def host_own(j, k):
+        c = host_of(j, k)
+        if known(k):
+            for q in range(pieces):
+                vec_wait(vec_from[c].index(k), q)
+            own = vec_in.at[vec_from[c].index(k)]
+        else:
+            for r in range(rounds):
+                landed(guest.at[k, few(r), :], guest_recv.at[k, r])
+            own = guest.at[k]
+        high, low = halves(own[...])
+        guest_stack[:height] = high
+        guest_stack[height:] = low
+
+        @pl.loop(0, pieces)
+        def _(q):
+            if c == j:
+                part_in[part_from[j].index(k), :, wide(q)] = products(height, q)
+            else:
+                guest_part[rounds, :, wide(q)] = products(height, q)
+
+        if c != j:
+            for r in range(rounds):
+                back(j, k, k, r).start()
 
     def make_part(c, block, q):
         slot, made = blocks[c].index(block), part_made[c].index(block)
@@ -580,29 +684,17 @@
         part_to(block, made, q).start()
 
     def take_before(c):
-        finish_serving(c)
-        for j, k in staying:
-            if j == c:
-                pl.when(a == k)(functools.partial(host, j, k))
         for block in before[c]:
             j, k = block
             slot, coming = blocks[c].index(block), vec_from[c].index(k)
-            if j != c:
-
-                def work(k=k):
-                    for q in range(pieces):
-                        vec_wait(coming, q)
-
-                if known(c, k) and (c, k) in staying:
-                    pl.when(a != k)(work)
-                else:
-                    work()
-                put(vec_in[coming])
-
-                @pl.loop(0, pieces)
-                def _(q):
-                    make_part(c, block, q)
-            else:
+            if both_down(block):
+                serving(c, early(columns - 3), lambda block: chunks)
+
+                @pl.when((a <= k) & (a > 0))
+                def _():
+                    @pl.loop(0, chunks)
+                    def _(i):
+                        serve_others(slot, block, i)
 
                 @pl.loop(0, chunks)
                 def _(i):
@@ -618,6 +710,51 @@
                     @pl.loop(0, pieces)
                     def _(n):
                         rest[:, wide(n)] -= nt3(stack[:, :WIDE], buf[slot, half, wide(n), at : at + WIDE])
+            elif j != c:
+                serving(c, early(columns - 3), lambda block: chunks)
+                for jj, kk in staying:
+                    if host_of(jj, kk) == c:
+                        pl.when(a == kk)(functools.partial(host, jj, kk))
+
+                def work():
+                    for q in range(pieces):
+                        vec_wait(coming, q)
+
+                if c == heir[k]:
+                    pl.when(a != k)(work)
+                else:
+                    work()
+                put(vec_in[coming])
+
+                @pl.loop(0, pieces)
+                def _(q):
+                    make_part(c, block, q)
+            else:
+                serving(c, early(columns - 3), early(columns - 2))
+                for q in range(pieces):
+                    vec_wait(coming, q)
+                put(vec_in[coming])
+
+                @pl.loop(0, pieces)
+                def _(q):
+                    @pl.when(a != k)
+                    def _():
+                        serve_ahead(slot, block, q, early(columns - 2)(block))
+
+                    for u in range(columns):
+                        for jj, kk in after[u]:
+                            if kk == c:
+
+                                @pl.when((a == kk) & (q == (chunks - EARLY[columns - 2] + 1) * TALL // WIDE + 1))
+                                def _():
+                                    pl.semaphore_signal(gate, inc=1, device_id=there(u), device_id_type=MESH)
+
+                    for n in range(WIDE // TALL):
+                        others(slot, block, q * (WIDE // TALL) + n)
+                    total = jnp.zeros((height, WIDE), jnp.float32)
+                    for half in range(side):
+                        total += nt3(stack[:, half * part : (half + 1) * part], buf[slot, half, wide(q), :])
+                    rest[:, wide(q)] -= total
 
     for c in range(columns):
         if before[c]:
@@ -636,10 +773,14 @@
                             part_wait(slot, q)
                         elif q == 0:
 
-                            @pl.when(a != k)
-                            def _():
+                            def back_wait(slot=slot):
                                 for r in range(rounds):
                                     landed(part_in.at[slot, few(r), :], back_recv.at[slot, r])
+
+                            if host_of(c, k) == c:
+                                pl.when(a != k)(back_wait)
+                            else:
+                                back_wait()
 
                         rest[:, here] -= part_in[slot, :, here]
 
@@ -654,26 +795,34 @@
         for c in range(columns):
             if vec_to[c]:
 
-                def work(c=c):
-                    for n in range(len(vec_to[c])):
-                        vec_out(c, n, q).start()
-
-                on(c, work)
-
-    def guests(c, act):
-        for n, (j, k) in enumerate([jk for jk in staying if jk[1] == c]):
-
-            def work():
+                on(c, functools.partial(vec_outs, c, q, lambda copy: copy.start()))
+
+    def guest_round(c, r):
+        def work():
+            if r:
+                guest_out(c, r - 1).wait_send()
+            if r < rounds:
+                guest_out(c, r).start()
+
+        if known(c):
+            pl.when(a != c)(work)
+        else:
+            work()
+
+    def guests(c):
+        for block in lift_to(c):
+
+            @pl.when(a < c)
+            def _():
                 for r in range(rounds):
-                    act(guest_out(n, j, k, r))
-
-            if known(j, k):
-                pl.when(a != k)(work)
-            else:
-                work()
+                    lift_out(block, r).start()
+
+        if heir[c] is not None:
+            for r in range(1 if after[c] else rounds + 1):
+                guest_round(c, r)
 
     for c in range(columns):
-        on(c, functools.partial(guests, c, lambda copy: copy.start()))
+        on(c, functools.partial(guests, c))
     store = pltpu.make_async_copy(vec, out_ref, out_sem)
     store.start()
     sums[column] = squares
@@ -685,22 +834,57 @@
     for step in range(1, columns):
         sum_out(step).start()
 
+    for j, k in staying:
+        if host_of(j, k) != j:
+            pl.when((column == host_of(j, k)) & (a == k))(functools.partial(host_own, j, k))
+
     def give_after(c):
         for block in after[c]:
-            slot, coming = blocks[c].index(block), vec_from[c].index(block[1])
-
-            @pl.loop(0, chunks - pieces)
-            def _(i):
-                serve(slot, block, i)
-
-            for q in range(pieces):
-                vec_wait(coming, q)
-            put(vec_in[coming])
-
-            @pl.loop(0, pieces)
-            def _(q):
-                serve(slot, block, chunks - pieces + q)
-                make_part(c, block, q)
+            j, k = block
+            slot, coming = blocks[c].index(block), vec_from[c].index(k)
+
+            if heir[c] is not None:
+                for r in range(1, rounds + 1):
+                    guest_round(c, r)
+
+                    @pl.when(a == k)
+                    def _():
+                        if r == 1:
+                            pl.semaphore_wait(gate, 1)
+
+                    @pl.when(a >= k)
+                    def _():
+                        @pl.loop((r - 1) * LATER // rounds, r * LATER // rounds)
+                        def _(i):
+                            serve(slot, block, i)
+
+            @pl.when(a >= k)
+            def _():
+                for q in range(pieces):
+                    vec_wait(coming, q)
+                put(vec_in[coming])
+
+                @pl.loop(0, pieces)
+                def _(q):
+                    serve_ahead(slot, block, q, LATER)
+                    make_part(c, block, q)
+
+            @pl.when(a == k)
+            def _():
+                for z in range(k):
+                    for r in range(rounds):
+                        landed(guest.at[z, few(r), :], guest_recv.at[z, r])
+                    high, low = halves(guest[z])
+                    stack[:height] = high
+                    stack[height:] = low
+
+                    @pl.loop(0, pieces)
+                    def _(q):
+                        total = jnp.zeros((height, WIDE), jnp.float32)
+                        for half in range(side):
+                            total += nt3(stack[:, half * part : (half + 1) * part], buf[slot, half, wide(q), :])
+                        guest[groups - 1 - z, :, wide(q)] = total
+                        lift_back(block, z, q).start()
 
     for c in range(columns):
         if after[c]:
@@ -715,20 +899,27 @@
 
         @pl.when((column == j) & (a == k))
         def _():
-            if t is None:
-                for q in range(pieces):
-                    for step in range(1, side):
-                        stay_out(step, q).wait_send()
-                for r in range(rounds):
-                    for z in range(groups):
-                        if z != k:
-                            back(j, k, z, r).wait_send()
-            elif t != j:
+            if t is not None and t != j:
 
                 @pl.loop(0, chunks)
                 def _(i):
                     entry(blocks[t].index((j, k)), i, t).wait_send()
 
+    for j, k in staying:
+
+        @pl.when((column == j) & (a == k))
+        def _():
+            for q in range(pieces):
+                for step in range(0 if host_of(j, k) != j else 1, side):
+                    stay_out(step, q, host_of(j, k)).wait_send()
+
+        @pl.when((column == host_of(j, k)) & (a == k))
+        def _():
+            for r in range(rounds):
+                for z in range(groups):
+                    if z != k or host_of(j, k) != j:
+                        back(j, k, z, r).wait_send()
+
     for c in range(columns):
 
         def work(c=c):
@@ -736,16 +927,33 @@
 
                 @pl.loop(0, chunks)
                 def _(i):
-                    flows(slot, block, i, lambda copy: copy.wait_send())
+                    line_flows(slot, block, i, lambda copy: copy.wait_send())
+                    side_flows(slot, block, i, lambda copy: copy.wait_send())
                     if both_down(block):
                         other_flows(slot, block, i, lambda copy: copy.wait_send())
 
             for q in range(pieces):
-                for n in range(len(vec_to[c])):
-                    vec_out(c, n, q).wait_send()
+                vec_outs(c, q, lambda copy: copy.wait_send())
                 for made, block in enumerate(part_made[c]):
-                    part_to(block, made, q).wait_send()
-            guests(c, lambda copy: copy.wait_send())
+                    if lifted(block):
+
+                        @pl.when(a >= block[1])
+                        def _():
+                            part_to(block, made, q).wait_send()
+
+                        @pl.when(a == block[1])
+                        def _():
+                            for z in range(block[1]):
+                                lift_back(block, z, q).wait_send()
+                    else:
+                        part_to(block, made, q).wait_send()
+            for block in lift_to(c):
+
+                @pl.when(a < c)
+                def _():
+                    for r in range(rounds):
+                        lift_out(block, r).wait_send()
+
 
         on(c, work)
     for step in range(1, columns):
@@ -769,7 +977,7 @@
     order = lax.dynamic_slice_in_dim(pivot_order, column * width, width)[None, :]
     live = (jnp.arange(height, dtype=jnp.int32) < row_count[0]).astype(jnp.float32)[:, None]
     slots = max([sum(target_of(j, k) == c for j in range(groups) for k in range(j)) for c in range(groups)])
-    chunks, pieces, rounds, chips = depth // TALL, width // WIDE, height // ROUND, groups // 2
+    chunks, pieces, rounds, chips = depth // TALL, width // WIDE, groups - 1, groups // 2
     sem, space = pltpu.SemaphoreType.DMA, pltpu.VMEM
     f32, bf16 = jnp.float32, jnp.bfloat16
     held = pl.BlockSpec(memory_space=pltpu.VMEM)
@@ -793,8 +1001,8 @@
             space((8, WIDE), bf16),
             space((side, depth, part), f32),
             space((groups, height, width), f32),
-            space((2 * groups * ROUND, width), bf16),
-            space((rounds, groups * ROUND, width), f32),
+            space((2 * height, width), bf16),
+            space((rounds + 1, height, width), f32),
             sem((chunks,)),
             sem((slots, side, chunks)),
             sem((slots, chunks)),
@@ -814,12 +1022,15 @@
             sem((groups,)),
             sem(()),
             sem(()),
-            sem((side - 1, pieces)),
             sem((side, pieces)),
+            sem((side, pieces)),
+            sem((rounds,)),
             sem((groups, rounds)),
             sem((groups, rounds)),
             sem((groups, rounds)),
-            sem((groups, rounds)),
+            sem((rounds,)),
+            sem((groups, pieces)),
+            pltpu.SemaphoreType.REGULAR,
         ],
         compiler_params=pltpu.CompilerParams(collective_id=0, has_side_effects=True, vmem_limit_bytes=60 * 1024 * 1024),
     )(slab, factor, block_inverse, order, live)
@@ -829,7 +1040,7 @@
 def per_device(slab, factor, block_inverse, pivot_order, row_count):
     groups, rows = lax.axis_size("cols"), lax.axis_size("rows")
     depth, part = factor.shape
-    fits = groups // 2 == 2 and rows % groups == 0 and rows > groups and part % WIDE == 0 and depth % WIDE == 0 and slab.shape[0] % ROUND == 0
+    fits = groups // 2 == 2 and rows % groups == 0 and rows > groups and part % WIDE == 0 and depth % WIDE == 0 and slab.shape[0] % (8 * (groups - 1)) == 0
     one = chain_device if fits else plain_device
     return one(slab, factor, block_inverse, pivot_order, row_count)
 

time: 184 us -> 168 us (0.913)
  the two profiles are of different devices: /device:TPU:0 before, /device:TPU:9 now
where the time goes in v1:
time: 168 us
  Pallas kernels  162 us (96%)
  local copies, waits for them, and re-layouts  4.31 us (3%)
    pallas_call x1, Pallas kernels, chain_device(): pl.pallas_call(functools.partial(chain_kernel, groups, side), out_shape=(...  162 us

profile of v1, /device:TPU:9, one launch (start us, length us, event | category | flops | bytes accessed | tf_op | source)
XLA Modules:
  0.0 167.9 jit_solution(307806101017616983)
XLA Ops:
  1.3 0.8 dynamic_slice.3
  2.1 0.6 broadcast_in_dim.4.order_ref
  2.7 0.7 fusion.live_ref
  3.3 161.6 %shard_map.68 = (f32[192,1536]{1,0:T(8,128)}, f32[1,192]{1,0:T(1,128)}) custom-call(f32[192,1536]{1,0:T(8,128)} %slab_ref.1, f32[1536,768]{1,0:T(8,128)} %factor_ref.1, f32[1536,1536]{1,0:T(8,128)} %inverse_ref.1, s32[1,1536]{1,0:T(1,128)} %broadcast_in_dim.4.order_ref, f32[192,1]{1,0:T(8,128)} %fusion.live_ref), custom_call_target="tpu_custom_call" | custom-call | tf_op jit(solution)/shard_map/pallas_call | solution.py:985
  165.0 0.0 copy-start
  165.0 2.4 %copy.10 = f32[192,1536]{1,0:T(8,128)} copy(f32[192,1536]{1,0:T(8,128)} %get-tuple-element.8) | data formatting | bytes 2359296
  167.3 0.0 copy-done
  167.3 0.6 copy.11
Async XLA Ops:
  165.0 2.4 %copy-start = (f32[1,192]{1,0:T(1,128)S(1)}, f32[1,192]{1,0:T(1,128)}, u32[]{:S(2)}) copy-start(f32[1,192]{1,0:T(1,128)} %get-tuple-element.5) | copy-start | bytes 2308
